TPU v7x, 32 devices: a whole 2x2x4 slice. The times are simulated.
32 devices in a mesh: front: 2 (over core), row: 4 (over y, x), col: 4 (over z).
Axes of the slice: x: 2, y: 2, z: 4, core: 2. Of those that a mesh axis runs over, the one named last changes fastest.
Arguments:
- front_rows: float32 [4096, 24576], P(('front', 'row'), 'col'), parts along dimension 0, may hold values from -0.0546875 to 0.0546875
- random_columns: bfloat16 [49152, 512], P(('front', 'col'), 'row'), parts along dimension 0, may hold values from -6 to 6
Outputs:
- basis: float32 [4096, 256], P(('front', 'row', 'col')), parts along dimension 0
- projected: float32 [1024, 512], P(('front', 'row')), parts along dimension 0
There are 2 independent parts, one for each index of `front`. A program takes and returns all parts, laid end to end along the dimension named above; each array names one. Nothing has to cross between parts.
All inputs are finite; a program needn't handle non-finite values.
Results may differ from a plain program's by a relative error of at most 0.0003.
Values may be sent and summed in bfloat16 or wider, within the bound.
A program may use at most 64 MiB of HBM per device.

v0:
```python
import functools

import jax
import jax.numpy as jnp
from jax import lax
from jax.experimental import pallas as pl
from jax.experimental.pallas import tpu as pltpu
from jax.sharding import PartitionSpec as P

RANK = 256
PANEL = 8
MESH = pl.DeviceIdType.MESH

OUT_X = (
    ((0, 0), (1, 0), (0, 1), (0, 0)),
    ((2, 1), (3, 1), (1, 0), (1, 1)),
    ((3, 0), (2, 0), (2, 0), (3, 0)),
)
OUT_Y = (
    ((0, 1), (0, 0), (2, 1), (0, 1)),
    ((1, 0), (1, 1), (1, 1), (3, 1)),
    ((3, 1), (2, 1), (3, 0), (2, 0)),
)
RELAY_X = ((0, 0, 1, 1), (0, 1, 1, 1), (1, 1, 0, 0))
RELAY_Y = ((0, 1, 0, 1), (0, 0, 1, 0), (0, 0, 1, 1))
ROUNDS = len(OUT_X)


def product(left, right, contract):
    return lax.dot_general(
        left,
        right,
        ((contract[:1], contract[1:]), ((), ())),
        precision=lax.Precision.HIGHEST,
        preferred_element_type=jnp.float32,
    )


def lookup(table, x, y):
    a, b, c, d = table
    return a + (b - a) * x + (c - a) * y + (a + d - b - c) * x * y


def factor(block, work):
    size = block.shape[0]
    rows = lax.broadcasted_iota(jnp.int32, (size, size), 0)
    lanes = lax.broadcasted_iota(jnp.int32, (size, size), 1)
    work[:, :size] = block
    work[:, size:] = jnp.where(rows == lanes, 1.0, 0.0).astype(jnp.float32)
    row_of = lax.broadcasted_iota(jnp.int32, (PANEL, 1), 0)
    for start in range(0, size, PANEL):
        panel = work[start : start + PANEL, :]
        for step in range(PANEL):
            column = panel[:, start + step : start + step + 1]
            scale = lax.rsqrt(column[step : step + 1, :])
            pivot = panel[step : step + 1, :] * scale
            weight = jnp.where(row_of > step, column * scale, 0.0)
            panel = jnp.where(row_of == step, pivot, panel - weight * pivot)
        work[start : start + PANEL, :] = panel
        if start + PANEL < size:
            tall = jnp.transpose(panel[:, :size])
            rest = work[start + PANEL :, :]
            for step in range(PANEL):
                rest = rest - tall[start + PANEL :, step : step + 1] * panel[step : step + 1, :]
            work[start + PANEL :, :] = rest
    return jnp.where(rows <= lanes, work[:, :size], 0.0), work[:, size:]


def kernel(
    cols,
    a_ref,
    om_ref,
    basis_ref,
    projected_ref,
    a32,
    high,
    low,
    om,
    part,
    rs_buf,
    sketch,
    gram,
    gram_in,
    t_own,
    t_in,
    t_sum,
    tr_buf,
    t_all,
    work,
    a_sem,
    om_sem,
    ring_send,
    ring_recv,
    rs_send,
    rs_recv,
    ag_send,
    ag_recv,
    g_send,
    g_recv,
    t_send,
    t_recv,
):
    _, chunks, depth, width = om_ref.shape
    ahead = min(2, (chunks - 1) // 4)
    own_rows = part.shape[1] // cols
    half = RANK // 2
    front, row, col = lax.axis_index("front"), lax.axis_index("row"), lax.axis_index("col")
    x, y = lax.rem(row, 2), lax.div(row, 2)
    beside = (front, row + 1 - 2 * x, col)
    above = (front, row + 2 - 4 * y, col)

    def along(step):
        return (front, row, lax.rem(col + step, cols))

    own_load = pltpu.make_async_copy(om_ref, om.at[pl.ds(2 * row, 2)], om_sem)
    own_load.start()

    def a_load(j):
        columns = pl.ds(pl.multiple_of(j * depth, depth), depth)
        return pltpu.make_async_copy(a_ref.at[:, columns], a32.at[j], a_sem.at[j])

    for i in range(chunks):
        for h in range(2):
            a_load(h * chunks + i).start()

    barrier = pltpu.get_barrier_semaphore()
    peers = [beside, above] + [along(step) for step in range(1, cols)]
    for peer in peers:
        pl.semaphore_signal(barrier, inc=1, device_id=peer, device_id_type=MESH)
    part[...] = jnp.zeros_like(part)
    own_load.wait()
    pl.semaphore_wait(barrier, len(peers))

    total_steps = ROUNDS * chunks + 4 * ahead
    lags = (
        ahead * lookup((3, 0, 2, 1), x, y),
        ahead * lookup((3, 2, 0, 1), x, y),
    )
    late = 4 * ahead * x * (1 - y)
    out_lag = ahead * x * y

    def pick(values, number):
        first, second, third = values
        middle = number * (2 - number)
        last = lax.div(number * (number - 1), 2)
        return first + (second - first) * middle + (third - first) * last

    def flipped(axis):
        return (1 - x, y) if axis == 0 else (x, 1 - y)

    def slots(axis, px, py):
        table = (OUT_X, OUT_Y)[axis]
        return [
            lookup([2 * block + side for block, side in entry], px, py)
            for entry in table
        ]

    leaving = [slots(axis, x, y) for axis in (0, 1)]
    coming = [slots(axis, *flipped(axis)) for axis in (0, 1)]
    relays = [
        [lookup(entry, x, y) for entry in table] for table in (RELAY_X, RELAY_Y)
    ]

    def hop(number, axis, i, slot):
        return pltpu.make_async_remote_copy(
            src_ref=om.at[slot, i],
            dst_ref=om.at[slot, i],
            send_sem=ring_send.at[number, axis, i],
            recv_sem=ring_recv.at[number, axis, i],
            device_id=(beside, above)[axis],
            device_id_type=MESH,
        )

    def accumulate(slot, i):
        block = lax.div(slot, 2)
        j = lax.rem(slot, 2) * chunks + i
        columns = om[slot, i]
        part[block] += jnp.dot(
            high[j], columns, preferred_element_type=jnp.float32
        ) + jnp.dot(low[j], columns, preferred_element_type=jnp.float32)

    def step_of(g, convert):
        found = []
        for axis in (0, 1):
            at = g - lags[axis]
            third = lax.div(at, 2 * chunks)
            at = at - late * third if axis == 0 else at
            live = jnp.logical_and(at >= 2 * chunks * third, at < ROUNDS * chunks)
            live = jnp.logical_and(g >= lags[axis], live)
            number = lax.div(at, chunks)
            i = lax.rem(at, chunks)
            slot = pick(coming[axis], number)
            relay = pick(relays[1 - axis], number)
            found.append((live, slot, i))

            @pl.when(live)
            def _():
                hop(number, axis, i, slot).wait_recv()

                @pl.when(relay == 1)
                def _():
                    hop(number, 1 - axis, i, slot).start()

        for axis in (0, 1):
            at = g + 1 - out_lag
            number = lax.div(at, chunks)
            i = lax.rem(at, chunks)
            relay = pick(relays[axis], number)
            due = jnp.logical_and(at >= chunks, at < ROUNDS * chunks)

            @pl.when(jnp.logical_and(due, relay == 0))
            def _():
                hop(number, axis, i, pick(leaving[axis], number)).start()

        if convert:
            for h in range(2):
                j = h * chunks + g
                a_load(j).wait()
                value = a32[j]
                near = value.astype(jnp.bfloat16)
                high[j] = near
                low[j] = (value - near.astype(jnp.float32)).astype(jnp.bfloat16)
            for h in range(2):
                accumulate(2 * row + h, g)
        for live, slot, i in found:

            @pl.when(live)
            def _():
                accumulate(slot, i)

    def launch():
        for axis in (0, 1):

            @pl.when(relays[axis][0] == 0)
            def _():
                @pl.loop(0, chunks)
                def _(i):
                    hop(0, axis, i, leaving[axis][0]).start()

    def gather(hooks):
        marks = sorted(set(hooks) | {chunks, total_steps})
        begin = 0
        for mark in marks:
            pl.loop(begin, mark)(functools.partial(step_of, convert=mark <= chunks))
            if mark in hooks:
                hooks[mark]()
            begin = mark

    def scatter(s, step):
        target = lax.rem(col + step, cols)
        rows = pl.ds(pl.multiple_of(target * own_rows, own_rows), own_rows)
        return pltpu.make_async_remote_copy(
            src_ref=part.at[s, rows],
            dst_ref=rs_buf.at[s, step - 1],
            send_sem=rs_send.at[s, step - 1],
            recv_sem=rs_recv.at[s, step - 1],
            device_id=along(step),
            device_id_type=MESH,
        )

    def spread(s, step, piece):
        return pltpu.make_async_remote_copy(
            src_ref=sketch.at[s, piece],
            dst_ref=sketch.at[s, piece],
            send_sem=ag_send.at[s, step - 1],
            recv_sem=ag_recv.at[s, step - 1],
            device_id=along(step),
            device_id_type=MESH,
        )

    def scatter_start(s):
        for step in range(1, cols):
            scatter(s, step).start()

    def scatter_end(s):
        rows = pl.ds(pl.multiple_of(col * own_rows, own_rows), own_rows)
        total = part[s, rows]
        for step in range(1, cols):
            scatter(s, step).wait_recv()
            total = total + rs_buf[s, step - 1]
        sketch[s, col] = total
        for step in range(1, cols):
            spread(s, step, col).start()

    def spread_end(s):
        for step in range(1, cols):
            spread(s, step, lax.rem(col + cols - step, cols)).wait_recv()
        return sketch[s].reshape(part.shape[1], width)

    def exchange(first, count):
        return pltpu.make_async_remote_copy(
            src_ref=gram.at[pl.ds(first, count)],
            dst_ref=gram_in.at[pl.ds(first, count)],
            send_sem=g_send.at[first],
            recv_sem=g_recv.at[first],
            device_id=beside,
            device_id_type=MESH,
        )

    def first_done():
        scatter_start(1)
        value = spread_end(0)
        gram[0] = product(value, value, (0, 0))
        exchange(0, 1).start()

    ready = chunks + 2 * ahead
    ready_next = 2 * chunks + 3 * ahead
    launch()
    gather({
        ready: lambda: scatter_start(0),
        (ready + ready_next) // 2: lambda: scatter_end(0),
        ready_next: first_done,
        min(ready_next + 7, total_steps): lambda: scatter_end(1),
    })

    first = sketch[0].reshape(part.shape[1], width)
    second = spread_end(1)
    gram[1] = product(first, second, (0, 0))
    gram[2] = product(second, second, (0, 0))
    exchange(1, 2).start()
    exchange(0, 1).wait_recv()
    upper_a, inverse_a = factor(gram[0] + gram_in[0], work)
    q_a = product(first, inverse_a, (1, 1))
    exchange(1, 2).wait_recv()
    across = product(inverse_a, gram[1] + gram_in[1], (1, 0))
    rest = second - product(q_a, across, (1, 0))
    for s in range(2):
        columns = slice(s * width, (s + 1) * width)
        t_own[0, :, columns] = product(q_a, part[2 + s], (0, 0))
        t_own[1, :, columns] = product(rest, part[2 + s], (0, 0))

    swap = pltpu.make_async_remote_copy(
        src_ref=t_own.at[1 - x],
        dst_ref=t_in,
        send_sem=t_send.at[0, 0],
        recv_sem=t_recv.at[0, 0],
        device_id=beside,
        device_id_type=MESH,
    )
    swap.start()
    schur = gram[2] + gram_in[2] - product(across, across, (0, 0))
    swap.wait_recv()
    t_rows = half // cols
    t_sum[...] = (t_own[x] + t_in[...]).reshape(t_sum.shape)

    def t_scatter(step):
        return pltpu.make_async_remote_copy(
            src_ref=t_sum.at[lax.rem(col + step, cols)],
            dst_ref=tr_buf.at[step - 1],
            send_sem=t_send.at[1, step - 1],
            recv_sem=t_recv.at[1, step - 1],
            device_id=along(step),
            device_id_type=MESH,
        )

    def t_spread(step, piece):
        return pltpu.make_async_remote_copy(
            src_ref=t_all.at[piece],
            dst_ref=t_all.at[piece],
            send_sem=t_send.at[2, step - 1],
            recv_sem=t_recv.at[2, step - 1],
            device_id=along(step),
            device_id_type=MESH,
        )

    for step in range(1, cols):
        t_scatter(step).start()
    total = t_sum[col]
    for step in range(1, cols):
        t_scatter(step).wait_recv()
        total = total + tr_buf[step - 1]
    t_all[col] = total
    for step in range(1, cols):
        t_spread(step, col).start()

    upper_b, inverse_b = factor(schur, work)
    mine_a = product(sketch[0, col], inverse_a, (1, 1))
    basis_ref[:, :half] = mine_a
    mine_b = sketch[1, col] - product(mine_a, across, (1, 0))
    basis_ref[:, half:] = product(mine_b, inverse_b, (1, 1))

    for step in range(1, cols):
        t_spread(step, lax.rem(col + cols - step, cols)).wait_recv()
    tail = t_all[...].reshape(half, 2 * width)
    is_low = x == 0
    projected_ref[:, :half] = jnp.where(is_low, upper_a, 0.0)
    projected_ref[:, half:RANK] = jnp.where(is_low, across, upper_b)
    projected_ref[:, RANK:] = jnp.where(is_low, tail, product(inverse_b, tail, (1, 0)))

    for number in range(ROUNDS):
        for axis in (0, 1):

            @pl.loop(0, chunks)
            def _(i):
                hop(number, axis, i, leaving[axis][number]).wait_send()

    for step in range(1, cols):
        for s in range(2):
            scatter(s, step).wait_send()
            spread(s, step, col).wait_send()
        t_scatter(step).wait_send()
        t_spread(step, col).wait_send()
    exchange(0, 1).wait_send()
    exchange(1, 2).wait_send()
    swap.wait_send()


def per_device(front_rows, random_columns):
    block_rows, depth = front_rows.shape
    width = random_columns.shape[1]
    cols = lax.axis_size("col")
    half = RANK // 2
    own_rows = block_rows // cols
    chunk = 256 if depth >= 4096 else 128
    chunks = depth // 2 // chunk
    columns = random_columns.reshape(2, chunks, chunk, width)
    vmem = pltpu.VMEM
    f32, bf16 = jnp.float32, jnp.bfloat16
    dma = pltpu.SemaphoreType.DMA
    return pl.pallas_call(
        functools.partial(kernel, cols),
        out_shape=(
            jax.ShapeDtypeStruct((own_rows, RANK), f32),
            jax.ShapeDtypeStruct((half, 4 * width), f32),
        ),
        in_specs=[pl.BlockSpec(memory_space=pl.ANY)] * 2,
        out_specs=(pl.BlockSpec(memory_space=pltpu.VMEM),) * 2,
        scratch_shapes=[
            vmem((2 * chunks, block_rows, chunk), f32),
            vmem((2 * chunks, block_rows, chunk), bf16),
            vmem((2 * chunks, block_rows, chunk), bf16),
            vmem((8, chunks, chunk, width), bf16),
            vmem((4, block_rows, width), f32),
            vmem((2, cols - 1, own_rows, width), f32),
            vmem((2, cols, own_rows, width), f32),
            vmem((3, half, half), f32),
            vmem((3, half, half), f32),
            vmem((2, half, 2 * width), f32),
            vmem((half, 2 * width), f32),
            vmem((cols, half // cols, 2 * width), f32),
            vmem((cols - 1, half // cols, 2 * width), f32),
            vmem((cols, half // cols, 2 * width), f32),
            vmem((half, RANK), f32),
            dma((2 * chunks,)),
            dma,
            dma((ROUNDS, 2, chunks)),
            dma((ROUNDS, 2, chunks)),
            dma((2, cols - 1)),
            dma((2, cols - 1)),
            dma((2, cols - 1)),
            dma((2, cols - 1)),
            dma((2,)),
            dma((2,)),
            dma((3, cols - 1)),
            dma((3, cols - 1)),
        ],
        compiler_params=pltpu.CompilerParams(
            collective_id=0, has_side_effects=True, vmem_limit_bytes=60 << 20
        ),
    )(front_rows, columns)


def solution(mesh):
    return jax.shard_map(
        per_device,
        mesh=mesh,
        in_specs=(P(("front", "row"), "col"), P(("front", "col"), "row")),
        out_specs=(P(("front", "row", "col"), None), P(("front", "row"), None)),
        check_vma=False,
    )
```

profile of v0, /device:TPU:0, one launch (start us, length us, event | category | flops | bytes accessed | tf_op | source)
XLA Modules:
  0.0 137.0 jit_solution(12216998158089557302)
XLA Ops:
  0.6 133.1 %shard_map.41 = (f32[128,256]{1,0:T(8,128)}, f32[128,512]{1,0:T(8,128)}) custom-call(f32[512,6144]{1,0:T(8,128)} %a_ref.1, bf16[2,12,256,128]{3,2,1,0:T(8,128)(2,1)} %bitcast.1), custom_call_target="tpu_custom_call" | custom-call | tf_op jit(solution)/shard_map/pallas_call | solution.py:420
  133.8 1.6 %copy.6 = f32[128,256]{1,0:T(8,128)} copy(f32[128,256]{1,0:T(8,128)} %get-tuple-element.4) | data formatting | bytes 262144
  135.3 1.7 %copy.7 = f32[128,512]{1,0:T(8,128)} copy(f32[128,512]{1,0:T(8,128)} %get-tuple-element.5) | data formatting | bytes 524288
where the time goes:
time: 137 us
  Pallas kernels  133 us (97%)
  local copies, waits for them, and re-layouts  3.24 us (2%)
    pallas_call x1, Pallas kernels, per_device(): pl.pallas_call(functools.partial(kernel, cols), out_shape=(jax.ShapeDtype...  133 us
    unnamed x2, local copies, waits for them, and re-layouts  3.24 us

commit v1 on v0

--- a/solution.py
+++ b/solution.py
@@ -9,21 +9,75 @@
 
 RANK = 256
 PANEL = 8
+CHUNK = 256
+LAG = 3
+FACTOR_LAG = 4
 MESH = pl.DeviceIdType.MESH
 
-OUT_X = (
-    ((0, 0), (1, 0), (0, 1), (0, 0)),
-    ((2, 1), (3, 1), (1, 0), (1, 1)),
-    ((3, 0), (2, 0), (2, 0), (3, 0)),
-)
-OUT_Y = (
-    ((0, 1), (0, 0), (2, 1), (0, 1)),
-    ((1, 0), (1, 1), (1, 1), (3, 1)),
-    ((3, 1), (2, 1), (3, 0), (2, 0)),
-)
-RELAY_X = ((0, 0, 1, 1), (0, 1, 1, 1), (1, 1, 0, 0))
-RELAY_Y = ((0, 1, 0, 1), (0, 0, 1, 0), (0, 0, 1, 1))
-ROUNDS = len(OUT_X)
+
+def send_plan(size, lag):
+    n, d = size, lag
+    x_runs = (
+        ((0, n, 0, 0), (n, n, 5, 0), (2 * n, 2 * d, 6, 0), (2 * n + 4 * d, n - 3 * d, 6, 2 * d)),
+        (
+            (0, n, 2, 0),
+            (n, 2 * d, 7, 0),
+            (n + 2 * d, d, 3, n - d),
+            (n + 3 * d, n - 2 * d, 7, 2 * d),
+            (2 * n + d, d, 4, 0),
+            (2 * n + 3 * d, n - 2 * d, 4, d),
+        ),
+        ((0, d, 4, 0), (d, n, 1, 0), (n + d, n, 2, 0), (2 * n + d, n - d, 4, d)),
+        ((0, 2 * d, 6, 0), (2 * d, n, 0, 0), (n + 2 * d, n, 3, 0), (2 * n + 2 * d, n - 2 * d, 6, 2 * d)),
+    )
+    y_runs = (
+        ((0, n, 1, 0), (n, n, 2, 0), (2 * n, n, 7, 0)),
+        ((0, d, 3, 0), (d, n, 0, 0), (n + d, n - d, 3, d), (2 * n, n, 5, 0)),
+        (
+            (0, n, 5, 0),
+            (n, 2 * d, 6, 0),
+            (n + 3 * d, n - d, 3, 0),
+            (2 * n + 2 * d, d, 4, n - d),
+            (2 * n + 3 * d, n - 2 * d, 6, 2 * d),
+        ),
+        (
+            (0, 2 * d, 7, 0),
+            (2 * d, n, 1, 0),
+            (n + 2 * d, n - 2 * d, 7, 2 * d),
+            (2 * n, d, 4, 0),
+            (2 * n + d, d, 6, n - d),
+            (2 * n + 2 * d, n - d, 4, d),
+        ),
+    )
+    taken = [{(2 * row + h, i): 0 for h in range(2) for i in range(n)} for row in range(4)]
+    for axis, runs_of in enumerate((x_runs, y_runs)):
+        for row, runs in enumerate(runs_of):
+            for start, length, slot, chunk in runs:
+                for i in range(length):
+                    taken[row ^ (1, 2)[axis]][slot, chunk + i] = start + i + d
+    plan = []
+    for runs_of in (x_runs, y_runs):
+        most = max(len(runs) for runs in runs_of)
+        table = []
+        for row, runs in enumerate(runs_of):
+            sent, free, rows = 0, 0, []
+            for start, length, slot, chunk in runs:
+                ready = [taken[row][slot, chunk + i] for i in range(length)]
+                at_once = max([free] + ready)
+                stream = max([free] + [when - i for i, when in enumerate(ready)])
+                if at_once <= stream or at_once <= start:
+                    issue, free = (at_once, 0, 0), at_once
+                else:
+                    issue, free = (-1, stream, stream + length), stream + length - 1
+                rows.append(
+                    (start, start + length, slot, chunk - start, sent - start, chunk, sent, length)
+                    + issue
+                )
+                sent += length
+            rows += [(0,) * 8 + (-1, 0, 0)] * (most - len(runs))
+            table.append((rows, sent))
+        plan.append(table)
+    return plan
 
 
 def product(left, right, contract):
@@ -63,11 +117,19 @@
             for step in range(PANEL):
                 rest = rest - tall[start + PANEL :, step : step + 1] * panel[step : step + 1, :]
             work[start + PANEL :, :] = rest
+        yield
+
+
+def factored(work):
+    size = work.shape[0]
+    rows = lax.broadcasted_iota(jnp.int32, (size, size), 0)
+    lanes = lax.broadcasted_iota(jnp.int32, (size, size), 1)
     return jnp.where(rows <= lanes, work[:, :size], 0.0), work[:, size:]
 
 
 def kernel(
     cols,
+    lag,
     a_ref,
     om_ref,
     basis_ref,
@@ -86,7 +148,8 @@
     t_sum,
     tr_buf,
     t_all,
-    work,
+    work_a,
+    work_b,
     a_sem,
     om_sem,
     ring_send,
@@ -101,7 +164,6 @@
     t_recv,
 ):
     _, chunks, depth, width = om_ref.shape
-    ahead = min(2, (chunks - 1) // 4)
     own_rows = part.shape[1] // cols
     half = RANK // 2
     front, row, col = lax.axis_index("front"), lax.axis_index("row"), lax.axis_index("col")
@@ -111,6 +173,9 @@
 
     def along(step):
         return (front, row, lax.rem(col + step, cols))
+
+    upper = lax.div(2 * col, cols)
+    outward = [step + upper * (cols - 2 * step) for step in range(cols - 1, 0, -1)]
 
     own_load = pltpu.make_async_copy(om_ref, om.at[pl.ds(2 * row, 2)], om_sem)
     own_load.start()
@@ -131,42 +196,35 @@
     own_load.wait()
     pl.semaphore_wait(barrier, len(peers))
 
-    total_steps = ROUNDS * chunks + 4 * ahead
-    lags = (
-        ahead * lookup((3, 0, 2, 1), x, y),
-        ahead * lookup((3, 2, 0, 1), x, y),
-    )
-    late = 4 * ahead * x * (1 - y)
-    out_lag = ahead * x * y
-
-    def pick(values, number):
-        first, second, third = values
-        middle = number * (2 - number)
-        last = lax.div(number * (number - 1), 2)
-        return first + (second - first) * middle + (third - first) * last
-
-    def flipped(axis):
-        return (1 - x, y) if axis == 0 else (x, 1 - y)
-
-    def slots(axis, px, py):
-        table = (OUT_X, OUT_Y)[axis]
+    plan = send_plan(chunks, lag)
+    total_steps = 3 * chunks + 2 * lag
+
+    def runs_at(axis, px, py):
+        table = plan[axis]
         return [
-            lookup([2 * block + side for block, side in entry], px, py)
-            for entry in table
+            [lookup([rows[k][field] for rows, _ in table], px, py) for field in range(11)]
+            for k in range(len(table[0][0]))
         ]
 
-    leaving = [slots(axis, x, y) for axis in (0, 1)]
-    coming = [slots(axis, *flipped(axis)) for axis in (0, 1)]
-    relays = [
-        [lookup(entry, x, y) for entry in table] for table in (RELAY_X, RELAY_Y)
-    ]
-
-    def hop(number, axis, i, slot):
+    leaving = [runs_at(axis, x, y) for axis in (0, 1)]
+    coming = [runs_at(0, 1 - x, y), runs_at(1, x, 1 - y)]
+
+    def chosen(runs, at):
+        live, slot, i, order = False, 0, 0, 0
+        for start, end, run_slot, run_chunk, run_order, *_ in runs:
+            inside = jnp.logical_and(at >= start, at < end)
+            live = jnp.logical_or(live, inside)
+            slot = jnp.where(inside, run_slot, slot)
+            i = jnp.where(inside, run_chunk + at, i)
+            order = jnp.where(inside, run_order + at, order)
+        return live, slot, i, order
+
+    def hop(axis, slot, i, order):
         return pltpu.make_async_remote_copy(
             src_ref=om.at[slot, i],
             dst_ref=om.at[slot, i],
-            send_sem=ring_send.at[number, axis, i],
-            recv_sem=ring_recv.at[number, axis, i],
+            send_sem=ring_send.at[axis, order],
+            recv_sem=ring_recv.at[axis, order],
             device_id=(beside, above)[axis],
             device_id_type=MESH,
         )
@@ -179,38 +237,35 @@
             high[j], columns, preferred_element_type=jnp.float32
         ) + jnp.dot(low[j], columns, preferred_element_type=jnp.float32)
 
+    def issue(axis, g):
+        for k, run in enumerate(leaving[axis]):
+            _, _, slot, _, _, chunk, sent, length, at_once, stream, stop = run
+            if any(rows[k][8] >= 0 for rows, _ in plan[axis]):
+
+                @pl.when(at_once == g)
+                def _():
+                    @pl.loop(0, length)
+                    def _(i):
+                        hop(axis, slot, chunk + i, sent + i).start()
+
+            if any(rows[k][10] > 0 for rows, _ in plan[axis]):
+
+                @pl.when(jnp.logical_and(g >= stream, g < stop))
+                def _():
+                    i = g - stream
+                    hop(axis, slot, chunk + i, sent + i).start()
+
     def step_of(g, convert):
         found = []
         for axis in (0, 1):
-            at = g - lags[axis]
-            third = lax.div(at, 2 * chunks)
-            at = at - late * third if axis == 0 else at
-            live = jnp.logical_and(at >= 2 * chunks * third, at < ROUNDS * chunks)
-            live = jnp.logical_and(g >= lags[axis], live)
-            number = lax.div(at, chunks)
-            i = lax.rem(at, chunks)
-            slot = pick(coming[axis], number)
-            relay = pick(relays[1 - axis], number)
+            live, slot, i, order = chosen(coming[axis], g - lag)
             found.append((live, slot, i))
 
             @pl.when(live)
             def _():
-                hop(number, axis, i, slot).wait_recv()
-
-                @pl.when(relay == 1)
-                def _():
-                    hop(number, 1 - axis, i, slot).start()
-
-        for axis in (0, 1):
-            at = g + 1 - out_lag
-            number = lax.div(at, chunks)
-            i = lax.rem(at, chunks)
-            relay = pick(relays[axis], number)
-            due = jnp.logical_and(at >= chunks, at < ROUNDS * chunks)
-
-            @pl.when(jnp.logical_and(due, relay == 0))
-            def _():
-                hop(number, axis, i, pick(leaving[axis], number)).start()
+                hop(axis, slot, i, order).wait_recv()
+
+            issue(1 - axis, g)
 
         if convert:
             for h in range(2):
@@ -228,22 +283,16 @@
             def _():
                 accumulate(slot, i)
 
-    def launch():
-        for axis in (0, 1):
-
-            @pl.when(relays[axis][0] == 0)
-            def _():
-                @pl.loop(0, chunks)
-                def _(i):
-                    hop(0, axis, i, leaving[axis][0]).start()
-
     def gather(hooks):
         marks = sorted(set(hooks) | {chunks, total_steps})
         begin = 0
         for mark in marks:
-            pl.loop(begin, mark)(functools.partial(step_of, convert=mark <= chunks))
-            if mark in hooks:
-                hooks[mark]()
+            if mark > begin + 1:
+                pl.loop(begin, mark)(functools.partial(step_of, convert=mark <= chunks))
+            elif mark > begin:
+                step_of(begin, convert=mark <= chunks)
+            for hook in hooks.get(mark, ()):
+                hook()
             begin = mark
 
     def scatter(s, step):
@@ -269,7 +318,7 @@
         )
 
     def scatter_start(s):
-        for step in range(1, cols):
+        for step in outward:
             scatter(s, step).start()
 
     def scatter_end(s):
@@ -279,7 +328,7 @@
             scatter(s, step).wait_recv()
             total = total + rs_buf[s, step - 1]
         sketch[s, col] = total
-        for step in range(1, cols):
+        for step in outward:
             spread(s, step, col).start()
 
     def spread_end(s):
@@ -297,37 +346,64 @@
             device_id_type=MESH,
         )
 
+    factor_a = []
+
     def first_done():
-        scatter_start(1)
         value = spread_end(0)
         gram[0] = product(value, value, (0, 0))
         exchange(0, 1).start()
 
-    ready = chunks + 2 * ahead
-    ready_next = 2 * chunks + 3 * ahead
-    launch()
-    gather({
-        ready: lambda: scatter_start(0),
-        (ready + ready_next) // 2: lambda: scatter_end(0),
-        ready_next: first_done,
-        min(ready_next + 7, total_steps): lambda: scatter_end(1),
-    })
+    def first_panel():
+        exchange(0, 1).wait_recv()
+        factor_a.append(factor(gram[0] + gram_in[0], work_a))
+        next(factor_a[0])
+
+    def next_panel():
+        for _ in range(per_step):
+            next(factor_a[0], None)
+
+    ready = chunks + 3 * lag
+    ready_next = 2 * chunks + 3 * lag
+    panel_step = min(ready_next + FACTOR_LAG, total_steps - 1)
+    panels = half // PANEL
+    per_step = -(-panels // (total_steps - panel_step))
+    hooks = {}
+    for at, hook in (
+        (ready, lambda: scatter_start(0)),
+        ((ready + ready_next) // 2, lambda: scatter_end(0)),
+        (ready_next, lambda: scatter_start(1)),
+        (ready_next, first_done),
+        (min(ready_next + chunks // 2, total_steps), lambda: scatter_end(1)),
+        (panel_step, first_panel),
+    ):
+        hooks.setdefault(at, []).append(hook)
+    for at in range(panel_step + 1, total_steps + 1):
+        hooks.setdefault(at, []).append(next_panel)
+    gather(hooks)
+    for _ in factor_a[0]:
+        pass
 
     first = sketch[0].reshape(part.shape[1], width)
+    upper_a, inverse_a = factored(work_a)
+    q_a = product(first, inverse_a, (1, 1))
+
+    def projection(left):
+        return jnp.concatenate(
+            [product(left, part[2 + s], (0, 0)) for s in range(2)], axis=1
+        )
+
+    t_own[0] = projection(q_a)
     second = spread_end(1)
     gram[1] = product(first, second, (0, 0))
+    exchange(1, 1).start()
     gram[2] = product(second, second, (0, 0))
-    exchange(1, 2).start()
-    exchange(0, 1).wait_recv()
-    upper_a, inverse_a = factor(gram[0] + gram_in[0], work)
-    q_a = product(first, inverse_a, (1, 1))
-    exchange(1, 2).wait_recv()
+    exchange(2, 1).start()
+    coarse = projection(second)
+    mine_a = product(sketch[0, col], inverse_a, (1, 1))
+    basis_ref[:, :half] = mine_a
+    exchange(1, 1).wait_recv()
     across = product(inverse_a, gram[1] + gram_in[1], (1, 0))
-    rest = second - product(q_a, across, (1, 0))
-    for s in range(2):
-        columns = slice(s * width, (s + 1) * width)
-        t_own[0, :, columns] = product(q_a, part[2 + s], (0, 0))
-        t_own[1, :, columns] = product(rest, part[2 + s], (0, 0))
+    t_own[1] = coarse - product(across, t_own[0], (0, 0))
 
     swap = pltpu.make_async_remote_copy(
         src_ref=t_own.at[1 - x],
@@ -338,9 +414,12 @@
         device_id_type=MESH,
     )
     swap.start()
+    exchange(2, 1).wait_recv()
     schur = gram[2] + gram_in[2] - product(across, across, (0, 0))
+    factor_b = factor(schur, work_b)
+    for _ in range(panels * 7 // 16):
+        next(factor_b)
     swap.wait_recv()
-    t_rows = half // cols
     t_sum[...] = (t_own[x] + t_in[...]).reshape(t_sum.shape)
 
     def t_scatter(step):
@@ -363,19 +442,19 @@
             device_id_type=MESH,
         )
 
-    for step in range(1, cols):
+    for step in outward:
         t_scatter(step).start()
+    for _ in factor_b:
+        pass
     total = t_sum[col]
     for step in range(1, cols):
         t_scatter(step).wait_recv()
         total = total + tr_buf[step - 1]
     t_all[col] = total
-    for step in range(1, cols):
+    for step in outward:
         t_spread(step, col).start()
 
-    upper_b, inverse_b = factor(schur, work)
-    mine_a = product(sketch[0, col], inverse_a, (1, 1))
-    basis_ref[:, :half] = mine_a
+    upper_b, inverse_b = factored(work_b)
     mine_b = sketch[1, col] - product(mine_a, across, (1, 0))
     basis_ref[:, half:] = product(mine_b, inverse_b, (1, 1))
 
@@ -387,12 +466,11 @@
     projected_ref[:, half:RANK] = jnp.where(is_low, across, upper_b)
     projected_ref[:, RANK:] = jnp.where(is_low, tail, product(inverse_b, tail, (1, 0)))
 
-    for number in range(ROUNDS):
-        for axis in (0, 1):
-
-            @pl.loop(0, chunks)
-            def _(i):
-                hop(number, axis, i, leaving[axis][number]).wait_send()
+    for axis in (0, 1):
+
+        @pl.loop(0, lookup([sent for _, sent in plan[axis]], x, y))
+        def _(order):
+            hop(axis, 0, 0, order).wait_send()
 
     for step in range(1, cols):
         for s in range(2):
@@ -401,7 +479,8 @@
         t_scatter(step).wait_send()
         t_spread(step, col).wait_send()
     exchange(0, 1).wait_send()
-    exchange(1, 2).wait_send()
+    exchange(1, 1).wait_send()
+    exchange(2, 1).wait_send()
     swap.wait_send()
 
 
@@ -411,14 +490,15 @@
     cols = lax.axis_size("col")
     half = RANK // 2
     own_rows = block_rows // cols
-    chunk = 256 if depth >= 4096 else 128
+    chunk = min(CHUNK, depth // 12 // 128 * 128)
     chunks = depth // 2 // chunk
+    lag = max(1, min(LAG, chunks // 4))
     columns = random_columns.reshape(2, chunks, chunk, width)
     vmem = pltpu.VMEM
     f32, bf16 = jnp.float32, jnp.bfloat16
     dma = pltpu.SemaphoreType.DMA
     return pl.pallas_call(
-        functools.partial(kernel, cols),
+        functools.partial(kernel, cols, lag),
         out_shape=(
             jax.ShapeDtypeStruct((own_rows, RANK), f32),
             jax.ShapeDtypeStruct((half, 4 * width), f32),
@@ -441,16 +521,17 @@
             vmem((cols - 1, half // cols, 2 * width), f32),
             vmem((cols, half // cols, 2 * width), f32),
             vmem((half, RANK), f32),
+            vmem((half, RANK), f32),
             dma((2 * chunks,)),
             dma,
-            dma((ROUNDS, 2, chunks)),
-            dma((ROUNDS, 2, chunks)),
+            dma((2, 3 * chunks + lag)),
+            dma((2, 3 * chunks + lag)),
             dma((2, cols - 1)),
             dma((2, cols - 1)),
             dma((2, cols - 1)),
             dma((2, cols - 1)),
-            dma((2,)),
-            dma((2,)),
+            dma((3,)),
+            dma((3,)),
             dma((3, cols - 1)),
             dma((3, cols - 1)),
         ],

time: 137 us -> 112 us (0.82)
  Pallas kernels: 133 us -> 108 us
    pallas_call x1, Pallas kernels: 133 us -> 108 us  [per_device(): pl.pallas_call(functools.partial(kernel, cols, lag), out_shape=(jax.Shape...]
where the time goes in v1:
time: 112 us; the launch traced here: 111 us
  Pallas kernels  108 us (96%)
  local copies, waits for them, and re-layouts  3.24 us (3%)
    pallas_call x1, Pallas kernels, per_device(): pl.pallas_call(functools.partial(kernel, cols, lag), out_shape=(jax.Shape...  108 us
    unnamed x2, local copies, waits for them, and re-layouts  3.24 us

profile of v1, /device:TPU:0, one launch (start us, length us, event | category | flops | bytes accessed | tf_op | source)
XLA Modules:
  0.0 111.5 jit_solution(11547300380074199750)
XLA Ops:
  0.6 107.6 %shard_map.41 = (f32[128,256]{1,0:T(8,128)}, f32[128,512]{1,0:T(8,128)}) custom-call(f32[512,6144]{1,0:T(8,128)} %a_ref.1, bf16[2,12,256,128]{3,2,1,0:T(8,128)(2,1)} %bitcast.1), custom_call_target="tpu_custom_call" | custom-call | tf_op jit(solution)/shard_map/pallas_call | solution.py:500
  108.2 1.6 %copy.6 = f32[128,256]{1,0:T(8,128)} copy(f32[128,256]{1,0:T(8,128)} %get-tuple-element.4) | data formatting | bytes 262144
  109.8 1.7 %copy.7 = f32[128,512]{1,0:T(8,128)} copy(f32[128,512]{1,0:T(8,128)} %get-tuple-element.5) | data formatting | bytes 524288

commit v2 on v1

--- a/solution.py
+++ b/solution.py
@@ -11,43 +11,31 @@
 PANEL = 8
 CHUNK = 256
 LAG = 3
-FACTOR_LAG = 4
+SUM_LAG = 6
+FACTOR_LAG = 3
+PANELS_A_STEP = 4
 MESH = pl.DeviceIdType.MESH
 
 
 def send_plan(size, lag):
     n, d = size, lag
     x_runs = (
-        ((0, n, 0, 0), (n, n, 5, 0), (2 * n, 2 * d, 6, 0), (2 * n + 4 * d, n - 3 * d, 6, 2 * d)),
+        ((0, n, 0, 0), (n, n, 5, 0), (2 * n, n, 4, 0)),
+        ((0, n, 2, 0), (n, n, 3, 0), (2 * n, n, 7, 0)),
+        ((0, d, 4, 0), (d, n, 1, 0), (n + d, n, 2, 0), (2 * n + d, n - d, 4, d)),
         (
-            (0, n, 2, 0),
-            (n, 2 * d, 7, 0),
-            (n + 2 * d, d, 3, n - d),
-            (n + 3 * d, n - 2 * d, 7, 2 * d),
-            (2 * n + d, d, 4, 0),
-            (2 * n + 3 * d, n - 2 * d, 4, d),
+            (0, 2 * d, 6, 0),
+            (2 * d, n, 0, 0),
+            (n + 2 * d, n - d, 3, 0),
+            (2 * n + d, n - 2 * d, 6, 2 * d),
+            (3 * n - d, d, 7, n - d),
         ),
-        ((0, d, 4, 0), (d, n, 1, 0), (n + d, n, 2, 0), (2 * n + d, n - d, 4, d)),
-        ((0, 2 * d, 6, 0), (2 * d, n, 0, 0), (n + 2 * d, n, 3, 0), (2 * n + 2 * d, n - 2 * d, 6, 2 * d)),
     )
     y_runs = (
-        ((0, n, 1, 0), (n, n, 2, 0), (2 * n, n, 7, 0)),
+        ((0, n, 1, 0), (n, n, 2, 0), (2 * n, d, 3, n - d), (2 * n + d, n - d, 7, 0)),
         ((0, d, 3, 0), (d, n, 0, 0), (n + d, n - d, 3, d), (2 * n, n, 5, 0)),
-        (
-            (0, n, 5, 0),
-            (n, 2 * d, 6, 0),
-            (n + 3 * d, n - d, 3, 0),
-            (2 * n + 2 * d, d, 4, n - d),
-            (2 * n + 3 * d, n - 2 * d, 6, 2 * d),
-        ),
-        (
-            (0, 2 * d, 7, 0),
-            (2 * d, n, 1, 0),
-            (n + 2 * d, n - 2 * d, 7, 2 * d),
-            (2 * n, d, 4, 0),
-            (2 * n + d, d, 6, n - d),
-            (2 * n + 2 * d, n - d, 4, d),
-        ),
+        ((0, n, 5, 0), (n, n, 4, 0), (2 * n, 2 * d, 6, 0), (2 * n + 2 * d, n - 2 * d, 6, 2 * d)),
+        ((0, 2 * d, 7, 0), (2 * d, n, 1, 0), (n + 2 * d, n - 2 * d, 7, 2 * d), (2 * n, n, 6, 0)),
     )
     taken = [{(2 * row + h, i): 0 for h in range(2) for i in range(n)} for row in range(4)]
     for axis, runs_of in enumerate((x_runs, y_runs)):
@@ -101,22 +89,44 @@
     lanes = lax.broadcasted_iota(jnp.int32, (size, size), 1)
     work[:, :size] = block
     work[:, size:] = jnp.where(rows == lanes, 1.0, 0.0).astype(jnp.float32)
-    row_of = lax.broadcasted_iota(jnp.int32, (PANEL, 1), 0)
+    row_of = lax.broadcasted_iota(jnp.int32, (PANEL, size), 0)
+
+    def wide(value):
+        return jnp.concatenate([value, value], axis=-1)
+
     for start in range(0, size, PANEL):
+        groups = (size - start) // PANEL
+        columns = [
+            jnp.broadcast_to(
+                work[start:, start + k : start + k + 1], (size - start, size)
+            ).reshape(groups, PANEL, size)
+            for k in range(PANEL)
+        ]
         panel = work[start : start + PANEL, :]
-        for step in range(PANEL):
-            column = panel[:, start + step : start + step + 1]
-            scale = lax.rsqrt(column[step : step + 1, :])
-            pivot = panel[step : step + 1, :] * scale
-            weight = jnp.where(row_of > step, column * scale, 0.0)
-            panel = jnp.where(row_of == step, pivot, panel - weight * pivot)
-        work[start : start + PANEL, :] = panel
-        if start + PANEL < size:
-            tall = jnp.transpose(panel[:, :size])
-            rest = work[start + PANEL :, :]
-            for step in range(PANEL):
-                rest = rest - tall[start + PANEL :, step : step + 1] * panel[step : step + 1, :]
-            work[start + PANEL :, :] = rest
+        rest = work[start + PANEL :, :].reshape(groups - 1, PANEL, 2 * size) if groups > 1 else None
+        diagonal = jnp.ones((PANEL, size), jnp.float32)
+        for k in range(PANEL):
+            head = columns[k][0]
+            pivot = jnp.broadcast_to(head[k : k + 1], (PANEL, size))
+            inverse = 1.0 / pivot
+            diagonal = jnp.where(row_of == k, pivot, diagonal)
+            weight = jnp.where(row_of > k, head, 0.0) * inverse
+            below = columns[k][1:] * inverse[None] if groups > 1 else None
+            for j in range(k + 1, PANEL):
+                along = jnp.broadcast_to(columns[j][0][k : k + 1], (PANEL, size))
+                top = columns[j][0] - weight * along
+                if groups > 1:
+                    low = columns[j][1:] - below * along[None]
+                    columns[j] = jnp.concatenate([top[None], low], axis=0)
+                else:
+                    columns[j] = top[None]
+            row = jnp.broadcast_to(panel[k : k + 1], (PANEL, 2 * size))
+            panel = panel - wide(weight) * row
+            if groups > 1:
+                rest = rest - wide(below) * row[None]
+        work[start : start + PANEL, :] = panel * wide(lax.rsqrt(diagonal))
+        if groups > 1:
+            work[start + PANEL :, :] = rest.reshape(size - start - PANEL, 2 * size)
         yield
 
 
@@ -197,7 +207,7 @@
     pl.semaphore_wait(barrier, len(peers))
 
     plan = send_plan(chunks, lag)
-    total_steps = 3 * chunks + 2 * lag
+    total_steps = 3 * chunks + lag
 
     def runs_at(axis, px, py):
         table = plan[axis]
@@ -359,24 +369,23 @@
         next(factor_a[0])
 
     def next_panel():
-        for _ in range(per_step):
+        for _ in range(PANELS_A_STEP):
             next(factor_a[0], None)
 
     ready = chunks + 3 * lag
-    ready_next = 2 * chunks + 3 * lag
-    panel_step = min(ready_next + FACTOR_LAG, total_steps - 1)
+    ready_next = 2 * chunks + 2 * lag
     panels = half // PANEL
-    per_step = -(-panels // (total_steps - panel_step))
+    panel_step = min(ready + 2 * SUM_LAG + FACTOR_LAG, total_steps)
     hooks = {}
     for at, hook in (
         (ready, lambda: scatter_start(0)),
-        ((ready + ready_next) // 2, lambda: scatter_end(0)),
+        (ready + SUM_LAG, lambda: scatter_end(0)),
         (ready_next, lambda: scatter_start(1)),
-        (ready_next, first_done),
-        (min(ready_next + chunks // 2, total_steps), lambda: scatter_end(1)),
+        (ready + 2 * SUM_LAG, first_done),
+        (ready_next + SUM_LAG, lambda: scatter_end(1)),
         (panel_step, first_panel),
     ):
-        hooks.setdefault(at, []).append(hook)
+        hooks.setdefault(min(at, total_steps), []).append(hook)
     for at in range(panel_step + 1, total_steps + 1):
         hooks.setdefault(at, []).append(next_panel)
     gather(hooks)
@@ -417,8 +426,8 @@
     exchange(2, 1).wait_recv()
     schur = gram[2] + gram_in[2] - product(across, across, (0, 0))
     factor_b = factor(schur, work_b)
-    for _ in range(panels * 7 // 16):
-        next(factor_b)
+    for _ in factor_b:
+        pass
     swap.wait_recv()
     t_sum[...] = (t_own[x] + t_in[...]).reshape(t_sum.shape)
 
@@ -444,8 +453,9 @@
 
     for step in outward:
         t_scatter(step).start()
-    for _ in factor_b:
-        pass
+    upper_b, inverse_b = factored(work_b)
+    mine_b = sketch[1, col] - product(mine_a, across, (1, 0))
+    basis_ref[:, half:] = product(mine_b, inverse_b, (1, 1))
     total = t_sum[col]
     for step in range(1, cols):
         t_scatter(step).wait_recv()
@@ -453,10 +463,6 @@
     t_all[col] = total
     for step in outward:
         t_spread(step, col).start()
-
-    upper_b, inverse_b = factored(work_b)
-    mine_b = sketch[1, col] - product(mine_a, across, (1, 0))
-    basis_ref[:, half:] = product(mine_b, inverse_b, (1, 1))
 
     for step in range(1, cols):
         t_spread(step, lax.rem(col + cols - step, cols)).wait_recv()

time: 112 us -> 93.5 us (0.83)
  Pallas kernels: 108 us -> 89.5 us
    pallas_call x1, Pallas kernels: 108 us -> 89.5 us  [per_device(): pl.pallas_call(functools.partial(kernel, cols, lag), out_shape=(jax.Shape...]
where the time goes in v2:
time: 93.5 us; the launch traced here: 93.3 us
  Pallas kernels  89.5 us (96%)
  local copies, waits for them, and re-layouts  3.24 us (3%)
    pallas_call x1, Pallas kernels, per_device(): pl.pallas_call(functools.partial(kernel, cols, lag), out_shape=(jax.Shape...  89.5 us
    unnamed x2, local copies, waits for them, and re-layouts  3.24 us

profile of v2, /device:TPU:0, one launch (start us, length us, event | category | flops | bytes accessed | tf_op | source)
XLA Modules:
  0.0 93.3 jit_solution(13875787463900506170)
XLA Ops:
  0.6 89.5 %shard_map.41 = (f32[128,256]{1,0:T(8,128)}, f32[128,512]{1,0:T(8,128)}) custom-call(f32[512,6144]{1,0:T(8,128)} %a_ref.1, bf16[2,12,256,128]{3,2,1,0:T(8,128)(2,1)} %bitcast.1), custom_call_target="tpu_custom_call" | custom-call | tf_op jit(solution)/shard_map/pallas_call | solution.py:506
  90.1 1.6 %copy.6 = f32[128,256]{1,0:T(8,128)} copy(f32[128,256]{1,0:T(8,128)} %get-tuple-element.4) | data formatting | bytes 262144
  91.7 1.7 %copy.7 = f32[128,512]{1,0:T(8,128)} copy(f32[128,512]{1,0:T(8,128)} %get-tuple-element.5) | data formatting | bytes 524288

commit v3 on v2

--- a/solution.py
+++ b/solution.py
@@ -12,7 +12,7 @@
 CHUNK = 256
 LAG = 3
 SUM_LAG = 6
-FACTOR_LAG = 3
+FACTOR_LAG = 9
 PANELS_A_STEP = 4
 MESH = pl.DeviceIdType.MESH
 
@@ -382,7 +382,7 @@
         (ready + SUM_LAG, lambda: scatter_end(0)),
         (ready_next, lambda: scatter_start(1)),
         (ready + 2 * SUM_LAG, first_done),
-        (ready_next + SUM_LAG, lambda: scatter_end(1)),
+        (ready_next + SUM_LAG - 1, lambda: scatter_end(1)),
         (panel_step, first_panel),
     ):
         hooks.setdefault(min(at, total_steps), []).append(hook)

time: 93.5 us -> 91.2 us (0.975)
  Pallas kernels: 89.5 us -> 87.2 us
    pallas_call x1, Pallas kernels: 89.5 us -> 87.2 us  [per_device(): pl.pallas_call(functools.partial(kernel, cols, lag), out_shape=(jax.Shape...]
where the time goes in v3:
time: 91.2 us; the launch traced here: 91.1 us
  Pallas kernels  87.2 us (96%)
  local copies, waits for them, and re-layouts  3.24 us (4%)
    pallas_call x1, Pallas kernels, per_device(): pl.pallas_call(functools.partial(kernel, cols, lag), out_shape=(jax.Shape...  87.2 us
    unnamed x2, local copies, waits for them, and re-layouts  3.24 us

profile of v3, /device:TPU:0, one launch (start us, length us, event | category | flops | bytes accessed | tf_op | source)
XLA Modules:
  0.0 91.1 jit_solution(9811049285769159989)
XLA Ops:
  0.6 87.2 %shard_map.41 = (f32[128,256]{1,0:T(8,128)}, f32[128,512]{1,0:T(8,128)}) custom-call(f32[512,6144]{1,0:T(8,128)} %a_ref.1, bf16[2,12,256,128]{3,2,1,0:T(8,128)(2,1)} %bitcast.1), custom_call_target="tpu_custom_call" | custom-call | tf_op jit(solution)/shard_map/pallas_call | solution.py:506
  87.8 1.6 %copy.6 = f32[128,256]{1,0:T(8,128)} copy(f32[128,256]{1,0:T(8,128)} %get-tuple-element.4) | data formatting | bytes 262144
  89.4 1.7 %copy.7 = f32[128,512]{1,0:T(8,128)} copy(f32[128,512]{1,0:T(8,128)} %get-tuple-element.5) | data formatting | bytes 524288
